TPU v7x, 32 devices: a whole 2x2x4 slice. The times are simulated.
32 devices in a mesh: rows: 4 (over y, x), cols: 2 (over core), slabs: 4 (over z).
Axes of the slice: x: 2, y: 2, z: 4, core: 2. Of those that a mesh axis runs over, the one named last changes fastest.
Arguments:
- field_values: float32 [16, 64, 512, 128], P('rows', 'cols', 'slabs'), may hold values from 0.5 to 2
- mobility: float32 [16, 64, 512, 128], P('rows', 'cols', 'slabs'), may hold values from 0.03 to 0.15
- source: float32 [16, 64, 512, 128], P('rows', 'cols', 'slabs'), may hold values from -0.2 to 0.2
Outputs:
- anomaly: float32 [16, 64, 512, 128], P('rows', 'cols', 'slabs')
- field_values_end: float32 [16, 64, 512, 128], P('rows', 'cols', 'slabs')
All inputs are finite; a program needn't handle non-finite values.
Results may differ from a plain program's by a relative error of at most 0.00002.
Values sent between devices are 32-bit elements; how exact they have to be, the bound alone decides.
No kernel may reach another device: no remote copies, remote signals or barrier semaphores. Data moves between devices by JAX's collectives and lax.ppermute only.
A program may use at most 128 MiB of HBM per device.

v0:
```python
import jax
import jax.numpy as jnp
from jax import lax
from jax.sharding import PartitionSpec as P

STEPS = 3


def padded_2(block, sides, width):
    for axis, dim in sides:
        count = lax.axis_size(axis)
        forward = [(i, i + 1) for i in range(count - 1)]
        forward.append((count - 1, 0))
        backward = [(target, source) for source, target in forward]
        low = lax.ppermute(
            lax.slice_in_dim(block, block.shape[dim] - width, None, axis=dim), axis, forward
        )
        high = lax.ppermute(lax.slice_in_dim(block, 0, width, axis=dim), axis, backward)
        block = jnp.concatenate([low, block, high], axis=dim)
    return block


def strip_edges(values, dims):
    for dim in dims:
        values = lax.slice_in_dim(values, 1, values.shape[dim] - 1, axis=dim)
    return values


def neighbour(values, dim, start, dims):
    others = [other for other in dims if other != dim]
    values = strip_edges(values, others)
    return lax.slice_in_dim(values, start, start + values.shape[dim] - 2, axis=dim)


def one_step(padded, mobility, source):
    middle = strip_edges(padded, (0, 1, 2))
    lower = [neighbour(padded, dim, 0, (0, 1, 2)) for dim in (0, 1, 2)]
    upper = [neighbour(padded, dim, 2, (0, 1, 2)) for dim in (0, 1, 2)]
    spread = lower[0] + upper[0] + lower[1] + upper[1] + lower[2] + upper[2] - 6.0 * middle
    return middle + mobility * spread + source


def per_device(field_values, mobility, source):
    for step in range(STEPS):
        padded = padded_2(field_values, (("rows", 0), ("cols", 1), ("slabs", 2)), 1)
        field_values = one_step(padded, mobility, source)
    count = field_values.shape[2] * lax.axis_size("slabs")
    guess = 1.0
    moved = field_values - guess
    totals, squares = lax.psum(
        (jnp.sum(moved, axis=2, keepdims=True), jnp.sum(moved * moved, axis=2, keepdims=True)),
        "slabs",
    )
    line_mean = guess + totals / count
    centred = field_values - line_mean
    line_variance = squares / count - totals / count * (totals / count)
    anomaly = centred * lax.rsqrt(line_variance + 0.0001)
    return (anomaly, field_values)


def solution(mesh):
    return jax.shard_map(
        per_device,
        mesh=mesh,
        in_specs=(
            P("rows", "cols", "slabs", None),
            P("rows", "cols", "slabs", None),
            P("rows", "cols", "slabs", None),
        ),
        out_specs=(P("rows", "cols", "slabs", None), P("rows", "cols", "slabs", None)),
        check_vma=False,
    )
```

profile of v0, /device:TPU:0, one launch (start us, length us, event | category | flops | bytes accessed | tf_op | source)
XLA Modules:
  0.0 467.1 jit_solution(14527361977251745829)
XLA Ops:
  7.2 0.0 all-reduce.3.cloned.1.call-start
  7.2 0.0 copy-start.3
  7.2 4.1 fusion.31
  11.3 3.0 collective-permute-start
  14.3 1.0 collective-permute-start.1
  15.2 46.5 %collective-permute-done = f32[1,32,128,128]{3,2,1,0:T(8,128)S(1)} collective-permute-done((f32[1,32,128,128]{3,2,1,0:T(8,128)S(1)}, f32[1,32,128,128]{3,2,1,0:T(8,128)S(1)}, u32[]{:S(2)}, u32[]{:S(2)}) %collective-permute-start) | collective-permute-done | bytes 2097184 | tf_op jit(solution)/shard_map/ppermute | solution.py:15
  61.7 1.3 copy-done.6
  63.0 0.2 constant_dynamic-update-slice_fusion.2
  63.2 1.1 constant_dynamic-update-slice_fusion.1
  64.4 41.8 %collective-permute-done.1 = f32[1,32,128,128]{3,2,1,0:T(8,128)} collective-permute-done((f32[1,32,128,128]{3,2,1,0:T(8,128)}, f32[1,32,128,128]{3,2,1,0:T(8,128)}, u32[]{:S(2)}, u32[]{:S(2)}) %collective-permute-start.1) | collective-permute-done | bytes 2097184 | tf_op jit(solution)/shard_map/ppermute | solution.py:18
  106.1 1.7 constant_dynamic-update-slice_fusion
  107.9 0.1 fusion.28
  108.0 0.1 collective-permute-start.2
  108.0 0.5 collective-permute-start.3
  108.5 1.2 collective-permute-done.2
  109.8 0.6 collective-permute-done.3
  110.3 0.1 pad_maximum_fusion.64
  110.5 3.7 collective-permute-start.5
  114.2 0.1 collective-permute-start.4
  114.2 3.7 collective-permute-done.5
  117.9 0.1 copy.23
  118.0 3.1 collective-permute-done.4
  121.1 0.1 copy.21
  121.2 26.7 %fusion.22 = f32[4,32,128,128]{3,2,1,0:T(8,128)S(1)} fusion(f32[4,32,128,128]{3,2,1,0:T(8,128)} %param.5, f32[4,32,128,128]{3,2,1,0:T(8,128)} %param.3, f32[4,32,128,128]{3,2,1,0:T(8,128)} %param.4, f32[6,34,1,128]{3,2,1,0:T(1,128)S(1)} %copy.23, f32[6,1,128,128]{3,2,1,0:T(8,128)S(1)} %collective-permute-done.3, f32[6,32,128,128]{3,2,1,0:T(8,128)} %copy-done.2, ...), kind=kLoop, calls=%fused_computation.59 | loop fusion | flops 41943040 | bytes 51326976 | tf_op jit(solution)/shard_map/add | solution.py:40
  147.9 0.0 copy-start.1
  147.9 0.5 fusion.30
  148.4 1.5 collective-permute-start.6
  149.9 1.4 collective-permute-start.7
  151.4 46.5 %collective-permute-done.6 = f32[1,32,128,128]{3,2,1,0:T(8,128)S(1)} collective-permute-done((f32[1,32,128,128]{3,2,1,0:T(8,128)S(1)}, f32[1,32,128,128]{3,2,1,0:T(8,128)S(1)}, u32[]{:S(2)}, u32[]{:S(2)}) %collective-permute-start.6) | collective-permute-done | bytes 2097184 | tf_op jit(solution)/shard_map/ppermute | solution.py:15
  197.8 42.0 %collective-permute-done.7 = f32[1,32,128,128]{3,2,1,0:T(8,128)S(1)} collective-permute-done((f32[1,32,128,128]{3,2,1,0:T(8,128)S(1)}, f32[1,32,128,128]{3,2,1,0:T(8,128)S(1)}, u32[]{:S(2)}, u32[]{:S(2)}) %collective-permute-start.7) | collective-permute-done | bytes 2097184 | tf_op jit(solution)/shard_map/ppermute | solution.py:18
  239.9 0.1 pad_maximum_fusion.51
  239.9 0.1 collective-permute-start.8
  240.0 0.5 collective-permute-start.9
  240.5 1.2 collective-permute-done.8
  241.7 0.6 collective-permute-done.9
  242.3 0.2 pad_maximum_fusion.61
  242.5 0.7 collective-permute-start.11
  243.2 1.4 collective-permute-start.10
  244.6 5.9 %collective-permute-done.11 = f32[6,34,1,128]{3,1,2,0:T(8,128)S(1)} collective-permute-done((f32[6,34,1,128]{3,1,2,0:T(8,128)S(1)}, f32[6,34,1,128]{3,1,2,0:T(8,128)S(1)}, u32[]{:S(2)}, u32[]{:S(2)}) %collective-permute-start.11) | collective-permute-done | bytes 104480 | tf_op jit(solution)/shard_map/ppermute | solution.py:18
  250.5 0.1 copy.27
  250.6 0.1 copy.25
  250.8 28.7 %fusion.13 = f32[4,32,128,128]{3,2,1,0:T(8,128)} fusion(f32[4,32,128,128]{3,2,1,0:T(8,128)} %param.5, f32[4,32,128,128]{3,2,1,0:T(8,128)} %copy-done.1, f32[4,32,128,128]{3,2,1,0:T(8,128)} %param.4, f32[6,34,1,128]{3,2,1,0:T(1,128)S(1)} %copy.27, f32[6,1,128,128]{3,2,1,0:T(8,128)S(1)} %collective-permute-done.9, ...), kind=kLoop, calls=%fused_computation.32 | loop fusion | flops 58720256 | bytes 38744064 | tf_op jit(solution)/shard_map/add | solution.py:40
  279.5 2.6 fusion.29
  282.1 1.5 collective-permute-start.12
  283.7 1.4 collective-permute-start.13
  285.1 46.5 %collective-permute-done.12 = f32[1,32,128,128]{3,2,1,0:T(8,128)S(1)} collective-permute-done((f32[1,32,128,128]{3,2,1,0:T(8,128)S(1)}, f32[1,32,128,128]{3,2,1,0:T(8,128)S(1)}, u32[]{:S(2)}, u32[]{:S(2)}) %collective-permute-start.12) | collective-permute-done | bytes 2097184 | tf_op jit(solution)/shard_map/ppermute | solution.py:15
  331.6 42.6 %collective-permute-done.13 = f32[1,32,128,128]{3,2,1,0:T(8,128)S(1)} collective-permute-done((f32[1,32,128,128]{3,2,1,0:T(8,128)S(1)}, f32[1,32,128,128]{3,2,1,0:T(8,128)S(1)}, u32[]{:S(2)}, u32[]{:S(2)}) %collective-permute-start.13) | collective-permute-done | bytes 2097184 | tf_op jit(solution)/shard_map/ppermute | solution.py:18
  374.2 0.1 pad_maximum_fusion.48
  374.2 0.1 collective-permute-start.14
  374.3 0.5 collective-permute-start.15
  374.8 1.2 collective-permute-done.14
  376.0 0.6 collective-permute-done.15
  376.6 0.1 pad_maximum_fusion.56
  376.8 3.6 collective-permute-start.17
  380.4 0.2 collective-permute-start.16
  380.6 3.5 collective-permute-done.17
  384.1 0.1 copy.31
  384.2 3.3 collective-permute-done.16
  387.5 0.1 copy.29
  387.6 29.7 %add_reduce_fusion = (f32[4,32,128]{2,1,0:T(8,128)}, f32[4,32,128]{2,1,0:T(8,128)}, f32[4,32,128,128]{3,2,1,0:T(8,128)}) fusion(f32[4,32,128,128]{3,2,1,0:T(8,128)} %param.5, f32[4,32,128,128]{3,2,1,0:T(8,128)} %fusion.13, f32[4,32,128,128]{3,2,1,0:T(8,128)} %param.4, f32[6,34,1,128]{3,2,1,0:T(1,128)S(1)} %copy.31, ...), kind=kLoop, calls=%fused_computation.75 | loop fusion | flops 67076096 | bytes 38875136 | tf_op jit(solution)/shard_map/reduce_sum | solution.py:51
  417.3 0.0 all-reduce.3.cloned.1.call-update
  417.3 33.2 %all-reduce.3.cloned.1.call-done = (f32[4,32,1,128]{3,1,0,2:T(8,128)}, f32[4,32,1,128]{3,1,0,2:T(8,128)}) async-done(((f32[4,32,1,128]{3,1,0,2:T(8,128)}, f32[4,32,1,128]{3,1,0,2:T(8,128)}), (f32[4,32,1,128]{3,1,0,2:T(8,128)}, f32[4,32,1,128]{3,1,0,2:T(8,128)})) %all-reduce.3.cloned.1.call-update) | async-done | bytes 131088 | tf_op jit(solution)/shard_map/psum | solution.py:50
  450.5 0.9 add_bitcast_fusion
  451.4 8.8 %subtract_multiply_fusion = f32[4,32,128,128]{3,2,1,0:T(8,128)} fusion(f32[4,32,128,128]{3,2,1,0:T(8,128)} %get-tuple-element.8, f32[4,32,128]{2,1,0:T(8,128)S(1)} %get-tuple-element.28, f32[4,32,128]{2,1,0:T(8,128)S(1)} %get-tuple-element.27), kind=kLoop, calls=%fused_computation.74 | loop fusion | flops 4194304 | bytes 16908288 | tf_op jit(solution)/shard_map/mul | solution.py:57
  (20 shorter events, 0.1 us)
Async XLA Ops:
  7.2 443.3 %all-reduce.3.cloned.1.call-start = ((), (), s32[]{:S(2)}) async-start(), calls=%async_computation | async-start | bytes 262144 | tf_op jit(solution)/shard_map/psum | solution.py:50
  7.2 56.0 %copy-start.3 = (f32[4,32,128,128]{3,2,1,0:T(8,128)S(1)}, f32[4,32,128,128]{3,2,1,0:T(8,128)}, u32[]{:S(2)}) copy-start(f32[4,32,128,128]{3,2,1,0:T(8,128)} %param.3) | copy-start | bytes 25165828
  11.3 50.4 %collective-permute-start = (f32[1,32,128,128]{3,2,1,0:T(8,128)S(1)}, f32[1,32,128,128]{3,2,1,0:T(8,128)S(1)}, u32[]{:S(2)}, u32[]{:S(2)}) collective-permute-start(f32[1,32,128,128]{3,2,1,0:T(8,128)S(1)} %get-tuple-element.26), channel_id=1, source_target_pairs={{0,8},{8,16},{16,24},{24,0},{1,9},{9,17},{17,25},{25,1},{2,10},{10... | collective-permute-start | bytes 6291464 | tf_op jit(solution)/shard_map/ppermute | solution.py:15
  14.3 91.9 %collective-permute-start.1 = (f32[1,32,128,128]{3,2,1,0:T(8,128)}, f32[1,32,128,128]{3,2,1,0:T(8,128)}, u32[]{:S(2)}, u32[]{:S(2)}) collective-permute-start(f32[1,32,128,128]{3,2,1,0:T(8,128)} %get-tuple-element.25), channel_id=1, source_target_pairs={{8,0},{16,8},{24,16},{0,24},{9,1},{17,9},{25,17},{1,25},{10,2},{18... | collective-permute-start | bytes 6291464 | tf_op jit(solution)/shard_map/ppermute | solution.py:18
  61.7 1.3 copy-start.6
  107.9 13.2 %copy-start.2 = (f32[6,32,128,128]{3,2,1,0:T(8,128)}, f32[6,32,128,128]{3,2,1,0:T(8,128)S(1)}, u32[]{:S(2)}) copy-start(f32[6,32,128,128]{3,2,1,0:T(8,128)S(1)} %constant_dynamic-update-slice_fusion) | copy-start | bytes 37748740
  107.9 13.3 %copy-start.7 = (f32[1,32,128,128]{3,2,1,0:T(8,128)S(1)}, f32[1,32,128,128]{3,2,1,0:T(8,128)}, u32[]{:S(2)}) copy-start(f32[1,32,128,128]{3,2,1,0:T(8,128)} %copy-done.6) | copy-start | bytes 6291460
  108.0 1.8 collective-permute-start.2
  108.0 2.3 collective-permute-start.3
  110.5 7.4 %collective-permute-start.5 = (f32[6,34,1,128]{3,1,2,0:T(8,128)S(1)}, f32[6,34,1,128]{3,1,2,0:T(8,128)S(1)}, u32[]{:S(2)}, u32[]{:S(2)}) collective-permute-start(f32[6,34,1,128]{3,1,2,0:T(8,128)S(1)} %copy.22), channel_id=1, source_target_pairs={{1,0},{2,1},{3,2},{0,3},{5,4},{6,5},{7,6},{4,7},{9,8},{10,9},{11,1... | collective-permute-start | bytes 313352 | tf_op jit(solution)/shard_map/ppermute | solution.py:18
  114.2 6.9 %collective-permute-start.4 = (f32[6,34,1,128]{3,1,2,0:T(8,128)S(1)}, f32[6,34,1,128]{3,1,2,0:T(8,128)S(1)}, u32[]{:S(2)}, u32[]{:S(2)}) collective-permute-start(f32[6,34,1,128]{3,1,2,0:T(8,128)S(1)} %copy.20), channel_id=1, source_target_pairs={{0,1},{1,2},{2,3},{3,0},{4,5},{5,6},{6,7},{7,4},{8,9},{9,10},{10,1... | collective-permute-start | bytes 313352 | tf_op jit(solution)/shard_map/ppermute | solution.py:15
  147.9 94.4 %copy-start.1 = (f32[4,32,128,128]{3,2,1,0:T(8,128)}, f32[4,32,128,128]{3,2,1,0:T(8,128)S(1)}, u32[]{:S(2)}) copy-start(f32[4,32,128,128]{3,2,1,0:T(8,128)S(1)} %fusion.22) | copy-start | bytes 25165828
  148.4 49.5 %collective-permute-start.6 = (f32[1,32,128,128]{3,2,1,0:T(8,128)S(1)}, f32[1,32,128,128]{3,2,1,0:T(8,128)S(1)}, u32[]{:S(2)}, u32[]{:S(2)}) collective-permute-start(f32[1,32,128,128]{3,2,1,0:T(8,128)S(1)} %get-tuple-element.23), channel_id=1, source_target_pairs={{0,8},{8,16},{16,24},{24,0},{1,9},{9,17},{17,25},{25,1},{2,10},{10... | collective-permute-start | bytes 6291464 | tf_op jit(solution)/shard_map/ppermute | solution.py:15
  149.9 89.9 %collective-permute-start.7 = (f32[1,32,128,128]{3,2,1,0:T(8,128)S(1)}, f32[1,32,128,128]{3,2,1,0:T(8,128)S(1)}, u32[]{:S(2)}, u32[]{:S(2)}) collective-permute-start(f32[1,32,128,128]{3,2,1,0:T(8,128)S(1)} %get-tuple-element.24), channel_id=1, source_target_pairs={{8,0},{16,8},{24,16},{0,24},{9,1},{17,9},{25,17},{1,25},{10,2},{18... | collective-permute-start | bytes 6291464 | tf_op jit(solution)/shard_map/ppermute | solution.py:18
  239.8 2.6 copy-start.5
  239.9 1.8 collective-permute-start.8
  240.0 2.3 collective-permute-start.9
  242.5 8.0 %collective-permute-start.11 = (f32[6,34,1,128]{3,1,2,0:T(8,128)S(1)}, f32[6,34,1,128]{3,1,2,0:T(8,128)S(1)}, u32[]{:S(2)}, u32[]{:S(2)}) collective-permute-start(f32[6,34,1,128]{3,1,2,0:T(8,128)S(1)} %copy.26), channel_id=1, source_target_pairs={{1,0},{2,1},{3,2},{0,3},{5,4},{6,5},{7,6},{4,7},{9,8},{10,9},{11,1... | collective-permute-start | bytes 313352 | tf_op jit(solution)/shard_map/ppermute | solution.py:18
  243.2 7.4 %collective-permute-start.10 = (f32[6,34,1,128]{3,1,2,0:T(8,128)S(1)}, f32[6,34,1,128]{3,1,2,0:T(8,128)S(1)}, u32[]{:S(2)}, u32[]{:S(2)}) collective-permute-start(f32[6,34,1,128]{3,1,2,0:T(8,128)S(1)} %copy.24), channel_id=1, source_target_pairs={{0,1},{1,2},{2,3},{3,0},{4,5},{5,6},{6,7},{7,4},{8,9},{9,10},{10,1... | collective-permute-start | bytes 313352 | tf_op jit(solution)/shard_map/ppermute | solution.py:15
  279.4 94.7 %copy-start = (f32[4,32,128,128]{3,2,1,0:T(8,128)S(1)}, f32[4,32,128,128]{3,2,1,0:T(8,128)}, u32[]{:S(2)}) copy-start(f32[4,32,128,128]{3,2,1,0:T(8,128)} %fusion.13) | copy-start | bytes 25165828
  282.1 49.5 %collective-permute-start.12 = (f32[1,32,128,128]{3,2,1,0:T(8,128)S(1)}, f32[1,32,128,128]{3,2,1,0:T(8,128)S(1)}, u32[]{:S(2)}, u32[]{:S(2)}) collective-permute-start(f32[1,32,128,128]{3,2,1,0:T(8,128)S(1)} %get-tuple-element.21), channel_id=1, source_target_pairs={{0,8},{8,16},{16,24},{24,0},{1,9},{9,17},{17,25},{25,1},{2,10},{10... | collective-permute-start | bytes 6291464 | tf_op jit(solution)/shard_map/ppermute | solution.py:15
  283.7 90.5 %collective-permute-start.13 = (f32[1,32,128,128]{3,2,1,0:T(8,128)S(1)}, f32[1,32,128,128]{3,2,1,0:T(8,128)S(1)}, u32[]{:S(2)}, u32[]{:S(2)}) collective-permute-start(f32[1,32,128,128]{3,2,1,0:T(8,128)S(1)} %get-tuple-element.22), channel_id=1, source_target_pairs={{8,0},{16,8},{24,16},{0,24},{9,1},{17,9},{25,17},{1,25},{10,2},{18... | collective-permute-start | bytes 6291464 | tf_op jit(solution)/shard_map/ppermute | solution.py:18
  374.2 2.6 copy-start.4
  374.2 1.8 collective-permute-start.14
  374.3 2.3 collective-permute-start.15
  376.8 7.3 %collective-permute-start.17 = (f32[6,34,1,128]{3,1,2,0:T(8,128)S(1)}, f32[6,34,1,128]{3,1,2,0:T(8,128)S(1)}, u32[]{:S(2)}, u32[]{:S(2)}) collective-permute-start(f32[6,34,1,128]{3,1,2,0:T(8,128)S(1)} %copy.30), channel_id=1, source_target_pairs={{1,0},{2,1},{3,2},{0,3},{5,4},{6,5},{7,6},{4,7},{9,8},{10,9},{11,1... | collective-permute-start | bytes 313352 | tf_op jit(solution)/shard_map/ppermute | solution.py:18
  380.4 7.1 %collective-permute-start.16 = (f32[6,34,1,128]{3,1,2,0:T(8,128)S(1)}, f32[6,34,1,128]{3,1,2,0:T(8,128)S(1)}, u32[]{:S(2)}, u32[]{:S(2)}) collective-permute-start(f32[6,34,1,128]{3,1,2,0:T(8,128)S(1)} %copy.28), channel_id=1, source_target_pairs={{0,1},{1,2},{2,3},{3,0},{4,5},{5,6},{6,7},{7,4},{8,9},{9,10},{10,1... | collective-permute-start | bytes 313352 | tf_op jit(solution)/shard_map/ppermute | solution.py:15
Sparse Core Ops, SparseCore 0:
  417.4 33.0 all-reduce.2
where the time goes:
time: 467 us
  waiting for transfers between devices  324 us (69%)
  other arithmetic  95.3 us (20%)
  starting transfers between devices  21.3 us (5%)
  between operations  14.3 us (3%)
  local copies, waits for them, and re-layouts  12.4 us (3%)
    ppermute x9, waiting for transfers between devices, padded_2(): lax.ppermute(lax.slice_in_dim(block, block.shape[dim] - width, None, axis...  149 us
    ppermute x9, waiting for transfers between devices, padded_2(): lax.ppermute(lax.slice_in_dim(block, 0, width, axis=dim), axis, backward)  141 us
    add x2, other arithmetic, one_step(): return middle + mobility * spread + source  55.3 us
    psum x1, waiting for transfers between devices, per_device(): lax.psum((jnp.sum(moved, axis=2, keepdims=True), jnp.sum(moved * moved, a...  33.2 us
    reduce_sum x1, other arithmetic, per_device(): jnp.sum(moved, axis=2, keepdims=True)  29.7 us
    ppermute x9, starting transfers between devices, padded_2(): lax.ppermute(lax.slice_in_dim(block, 0, width, axis=dim), axis, backward)  13.3 us
  transfers between devices with their start and end apart: 19, of which 18 were waited for; matrix products, arithmetic and copies ran while one was open for 0% of the time, Pallas kernels for 0%

commit v1 on v0

v1 whole, which is shorter than its diff:
```python
import functools

import jax
import jax.numpy as jnp
from jax import lax
from jax.experimental import pallas as pl
from jax.experimental.pallas import tpu as pltpu
from jax.sharding import PartitionSpec as P

STEPS = 3
EPSILON = 0.0001
HEAD = 8
TAIL = 16
VMEM_BYTES = 12 * 2**20
OUTPUTS = {"step": 3, "last": 3, "partial": 2}


def ring(axis, shift):
    count = lax.axis_size(axis)
    return [(i, (i + shift) % count) for i in range(count)]


def shifted(block, axis, shift):
    return lax.ppermute(block, axis, ring(axis, shift))


def rows_per_block(*sizes):
    for rows in (8, 4, 2):
        if all(size % rows == 0 for size in sizes):
            return rows
    return 1


def plane_spec(source, rows, start):
    if isinstance(source, tuple):
        array, plane = source
        return array, pl.BlockSpec((None, rows) + array.shape[2:], lambda i: (plane, start(i), 0, 0))
    return source, pl.BlockSpec((rows,) + source.shape[1:], lambda i: (start(i), 0, 0))


def call(body, grid, specs, out_specs, out_shape, aliases, flops):
    bytes_accessed = sum(4 * s.size for s in out_shape)
    return pl.pallas_call(
        body,
        grid=grid,
        in_specs=[spec for _, spec in specs],
        out_specs=out_specs,
        out_shape=out_shape,
        input_output_aliases=aliases,
        cost_estimate=pl.CostEstimate(flops=flops, bytes_accessed=bytes_accessed, transcendentals=0),
        compiler_params=pltpu.CompilerParams(vmem_limit_bytes=VMEM_BYTES),
    )(*[array for array, _ in specs])


def token_spec():
    return jax.ShapeDtypeStruct((8, 128), jnp.float32), pl.BlockSpec((8, 128), lambda i: (0, 0))


def anywhere(arrays):
    return [(array, pl.BlockSpec(memory_space=pl.ANY)) for array in arrays]


def stencil_row(j, rows, sides, refs):
    center, before, after, mobility, source, x_low, x_high, z_low, z_high = refs
    i = pl.program_id(0)
    last = pl.num_programs(0) - 1
    middle = center[j]
    depth = middle.shape[0]
    left = center[j - 1] if j > 0 else jnp.where(i == 0, x_low[...], before[0])
    right = center[j + 1] if j < rows - 1 else jnp.where(i == last, x_high[...], after[0])
    z = lax.broadcasted_iota(jnp.int32, middle.shape, 0)
    lower = jnp.where(z == 0, z_low[j : j + 1, :], pltpu.roll(middle, 1, 0))
    upper = jnp.where(z == depth - 1, z_high[j : j + 1, :], pltpu.roll(middle, depth - 1, 0))
    spread = left + right + lower + upper - 6.0 * middle
    for side in sides:
        spread = spread + side[j]
    return middle + mobility[j] * spread + source[j]


def write_stats(stats, j, value):
    mean = jnp.sum(value, axis=0, keepdims=True) * (1.0 / value.shape[0])
    off = value - mean
    stats[0, j : j + 1, :] = mean
    stats[1, j : j + 1, :] = jnp.sum(off * off, axis=0, keepdims=True)


def update_body(*refs, rows, sides, kind):
    beside, ins = refs[:sides], refs[sides : sides + 9]
    outs = refs[-OUTPUTS[kind] :]
    for j in range(rows):
        value = stencil_row(j, rows, beside, ins)
        outs[0][j] = value
        if kind == "step":
            outs[1][j : j + 1, :] = value[:1]
            outs[2][j : j + 1, :] = value[-1:]
        if kind == "last":
            write_stats(outs[1], j, value)
            outs[2][j] = value
        if kind == "partial":
            outs[1][j] = ins[3][j]


def update(plane, sides, center, mobility, source, x_halo, z_halo, kind, end=()):
    size, depth, levels = mobility.shape[1:]
    rows = rows_per_block(size)
    same = lambda i: i
    specs = [plane_spec(side, rows, same) for side in sides]
    specs += [
        plane_spec(center, rows, same),
        plane_spec(center, 1, lambda i: jnp.maximum(i * rows - 1, 0)),
        plane_spec(center, 1, lambda i: jnp.minimum(i * rows + rows, size - 1)),
        plane_spec((mobility, plane), rows, same),
        plane_spec((source, plane), rows, same),
    ]
    specs += [(h, pl.BlockSpec((None, depth, levels), lambda i: (plane, 0, 0))) for h in x_halo]
    specs += [(h, pl.BlockSpec((None, rows, levels), lambda i: (plane, i, 0))) for h in z_halo]
    out_shape = [jax.ShapeDtypeStruct((size, depth, levels), jnp.float32)]
    out_specs = [pl.BlockSpec((rows, depth, levels), lambda i: (i, 0, 0))]
    aliases = {}
    if kind == "partial":
        out_shape, out_specs = out_shape * 2, out_specs * 2
    if kind == "last":
        out_shape += [jax.ShapeDtypeStruct((2, size, levels), jnp.float32)]
        out_specs += [pl.BlockSpec((2, rows, levels), lambda i: (0, i, 0))]
        out_shape += [jax.ShapeDtypeStruct(mobility.shape, jnp.float32)]
        out_specs += [pl.BlockSpec((None, rows, depth, levels), lambda i: (plane, i, 0, 0))]
        aliases = {len(specs) + k: 2 for k in range(len(end))}
        specs += anywhere(end)
    if kind == "step":
        out_shape += [jax.ShapeDtypeStruct((size, levels), jnp.float32)] * 2
        out_specs += [pl.BlockSpec((rows, levels), lambda i: (i, 0))] * 2
    body = functools.partial(update_body, rows=rows, sides=len(sides), kind=kind)
    return call(body, (size // rows,), specs, out_specs, out_shape, aliases, 20 * size * depth * levels)


def finish_body(*refs, rows):
    partial, mobility, side = refs[:3]
    out, stats = refs[-2:]
    for j in range(rows):
        value = partial[j] + mobility[j] * side[j]
        out[j] = value
        write_stats(stats, j, value)


def finish(start, partial, mobility, side, after):
    size, depth, levels = side.shape
    rows = rows_per_block(size, start)
    first = start // rows
    specs = [
        plane_spec(partial, rows, lambda i: first + i),
        plane_spec(mobility, rows, lambda i: first + i),
        plane_spec(side, rows, lambda i: i),
    ]
    specs += anywhere(after)
    out_shape = [
        jax.ShapeDtypeStruct((size, depth, levels), jnp.float32),
        jax.ShapeDtypeStruct((2, size, levels), jnp.float32),
    ]
    out_specs = [
        pl.BlockSpec((rows, depth, levels), lambda i: (i, 0, 0)),
        pl.BlockSpec((2, rows, levels), lambda i: (0, i, 0)),
    ]
    body = functools.partial(finish_body, rows=rows)
    return call(body, (size // rows,), specs, out_specs, out_shape, {}, 8 * size * depth * levels)


def scale_body(*refs, slabs):
    field, stats = refs[0], refs[1 : 1 + slabs]
    anomaly, token = refs[-2:]
    token[...] = jnp.zeros_like(token)
    rows, depth = field.shape[:2]
    mean = sum(s[0] for s in stats) * (1.0 / slabs)
    total = sum(s[1] for s in stats)
    for s in stats:
        off = s[0] - mean
        total = total + depth * (off * off)
    scale = lax.rsqrt(total * (1.0 / (depth * slabs)) + EPSILON)
    for j in range(rows):
        anomaly[j] = (field[j] - mean[j : j + 1, :]) * scale[j : j + 1, :]


def gathered(stats):
    parts = [stats]
    for shift in range(1, lax.axis_size("slabs")):
        parts.append(shifted(stats, "slabs", shift))
    return parts


def store_body(source, *refs):
    refs[-1][...] = source[...]


def stored(plane, start, whole, field, outs):
    size, depth, levels = field.shape
    rows = rows_per_block(size, start)
    first = start // rows
    specs = [plane_spec(field, rows, lambda i: i)] + anywhere(outs)
    out_specs = [pl.BlockSpec((None, rows, depth, levels), lambda i: (plane, first + i, 0, 0))]
    out_shape = [jax.ShapeDtypeStruct(whole, jnp.float32)]
    aliases = {1 + k: k for k in range(len(outs))}
    return call(store_body, (size // rows,), specs, out_specs, out_shape, aliases, 0)


def scaled(plane, start, whole, field, stats, outs):
    size, depth, levels = field.shape
    rows = rows_per_block(size, start)
    first = start // rows
    slabs = len(stats)
    specs = [plane_spec(field, rows, lambda i: i)]
    specs += [(s, pl.BlockSpec((2, rows, levels), lambda i: (0, i, 0))) for s in stats]
    specs += anywhere(outs)
    token_shape, token = token_spec()
    out_specs = [pl.BlockSpec((None, rows, depth, levels), lambda i: (plane, first + i, 0, 0)), token]
    out_shape = [jax.ShapeDtypeStruct(whole, jnp.float32), token_shape]
    aliases = {1 + slabs + k: k for k in range(len(outs))}
    body = functools.partial(scale_body, slabs=slabs)
    return call(body, (size // rows,), specs, out_specs, out_shape, aliases, 4 * size * depth * levels)


def copy_body(source, *refs, plane, start):
    pltpu.sync_copy(source.at[plane, pl.ds(start, refs[-2].shape[0])], refs[-2])
    refs[-1][...] = jnp.zeros_like(refs[-1])


def copied(array, plane, start, size, after):
    token_shape, _ = token_spec()
    specs = [(array, pl.BlockSpec(memory_space=pltpu.HBM))] + anywhere(after)
    out_shape = [jax.ShapeDtypeStruct((size,) + array.shape[2:], jnp.float32), token_shape]
    out_specs = [pl.BlockSpec(memory_space=pltpu.VMEM)] * 2
    body = functools.partial(copy_body, plane=plane, start=start)
    return call(body, (), specs, out_specs, out_shape, {}, 0)


def per_device(field, mobility, source):
    planes, size, depth, _ = field.shape
    top = planes - 1
    edges = field
    field, mobility, source = (pltpu.with_memory_space_constraint(a, pltpu.HBM) for a in (field, mobility, source))
    now = [(field, p) for p in range(planes)]
    head = HEAD if size > HEAD else 0
    opening = []
    token = ()
    for start, stop in ((0, head), (head, size)):
        if start < stop:
            part, *token = copied(field, top, start, stop - start, token)
            opening.append(shifted(part, "rows", 1))
    up = jnp.concatenate(opening) if head else opening[0]
    lows, _ = copied(field, 0, 0, size, token)
    down = shifted(lows, "rows", -1)
    x_edges = (edges[:, size - 1], edges[:, 0])
    z_edges = (edges[:, :, depth - 1], edges[:, :, 0])
    for step in range(STEPS - 1):
        x_halo = (shifted(x_edges[0], "cols", 1), shifted(x_edges[1], "cols", -1))
        z_halo = (shifted(z_edges[0], "slabs", 1), shifted(z_edges[1], "slabs", -1))
        new = {}
        order = [0, top] if step % 2 == 0 else [top, 0]
        for p in list(range(1, top)) + order:
            sides = (up if p == 0 else now[p - 1], down if p == top else now[p + 1])
            new[p] = update(p, sides, now[p], mobility, source, x_halo, z_halo, "step")
        cut = size - TAIL if step == STEPS - 2 else size
        sent = {}
        for p in order:
            value = new[p][0]
            parts = [value] if cut == size or p == order[0] else [value[:cut], value[cut:]]
            sent[p] = [shifted(part, "rows", -1 if p == 0 else 1) for part in parts]
        if cut == size:
            down, up = sent[0][0], sent[top][0]
        now = [new[p][0] for p in range(planes)]
        x_edges = (jnp.stack([v[size - 1] for v in now]), jnp.stack([v[0] for v in now]))
        z_edges = tuple(jnp.stack([new[p][k] for p in range(planes)]) for k in (2, 1))

    x_halo = (shifted(x_edges[0], "cols", 1), shifted(x_edges[1], "cols", -1))
    z_halo = (shifted(z_edges[0], "slabs", 1), shifted(z_edges[1], "slabs", -1))
    early, late = (top, 0) if STEPS % 2 == 0 else (0, top)
    outs, end = (), ()
    for p in list(range(1, top)) + [early]:
        sides = [now[q] for q in (p - 1, p + 1) if 0 <= q <= top]
        sides += sent[order[0]] if p == early else []
        value, stats, *end = update(p, sides, now[p], mobility, source, x_halo, z_halo, "last", end)
        stats = gathered(stats)
        *outs, token = scaled(p, 0, field.shape, value, stats, outs)
    inner = [now[1 if late == 0 else top - 1]]
    partial, late_mobility = update(late, inner, now[late], mobility, source, x_halo, z_halo, "partial")
    start = 0
    for side in sent[order[1]]:
        value, stats = finish(start, partial, late_mobility, side, (token,))
        stats = gathered(stats)
        *outs, token = scaled(late, start, field.shape, value, stats, outs)
        end = stored(late, start, field.shape, value, end)
        start += side.shape[0]
    return (*outs, *end)


def solution(mesh):
    spec = P("rows", "cols", "slabs", None)

    return jax.shard_map(per_device, mesh=mesh, in_specs=(spec, spec, spec), out_specs=(spec, spec), check_vma=False)
```

time: 467 us -> 300 us (0.64)
  waiting for transfers between devices: 324 us -> 186 us
  other arithmetic: 95.3 us -> 0.32 us
  Pallas kernels: 0 us -> 66.6 us
  starting transfers between devices: 21.3 us -> 42.6 us
  between operations: 14.3 us -> 0.9 us
  local copies, waits for them, and re-layouts: 12.4 us -> 2.67 us
    ppermute x18 -> x35, waiting for transfers between devices: 291 us -> 186 us  [shifted(): return lax.ppermute(block, axis, ring(axis, shift))]
    pallas_call x0 -> x24, Pallas kernels: none -> 66.6 us  [call(): pl.pallas_call(body, grid=grid, in_specs=[spec for _, spec in specs], out...]
    add x2 -> x0, other arithmetic: 55.3 us -> none  [one_step(): return middle + mobility * spread + source]
    psum x1 -> x0, waiting for transfers between devices: 33.2 us -> none  [per_device(): lax.psum((jnp.sum(moved, axis=2, keepdims=True), jnp.sum(moved * moved, a...]
    reduce_sum x1 -> x0, other arithmetic: 29.7 us -> none  [per_device(): jnp.sum(moved, axis=2, keepdims=True)]
    ppermute x18 -> x35, starting transfers between devices: 21.2 us -> 42.6 us  [shifted(): return lax.ppermute(block, axis, ring(axis, shift))]
    mul x1 -> x0, other arithmetic: 8.85 us -> none  [per_device(): anomaly = centred * lax.rsqrt(line_variance + 0.0001)]
    slice x10 -> x9, local copies, waits for them, and re-layouts: 7.32 us -> 1.6 us  [the longest x1 1.3 us: per_device(): z_edges = (edges[:, :, depth - 1], edges[:, :, 0])]
  transfers between devices with their start and end apart: 19 -> 35, of which waited for: 18 -> 18; matrix products, arithmetic and copies ran while one was open for 0% -> 1% of each run, Pallas kernels for 0% -> 21%
where the time goes in v1:
time: 300 us; the launch traced here: 299 us
  waiting for transfers between devices  186 us (62%)
  Pallas kernels  66.6 us (22%)
  starting transfers between devices  42.6 us (14%)
    ppermute x35, waiting for transfers between devices, shifted(): return lax.ppermute(block, axis, ring(axis, shift))  186 us
    pallas_call x24, Pallas kernels, call(): pl.pallas_call(body, grid=grid, in_specs=[spec for _, spec in specs], out...  66.6 us
    ppermute x35, starting transfers between devices, shifted(): return lax.ppermute(block, axis, ring(axis, shift))  42.6 us
  transfers between devices with their start and end apart: 35, of which 18 were waited for; matrix products, arithmetic and copies ran while one was open for 1% of the time, Pallas kernels for 21%

profile of v1, /device:TPU:0, one launch (start us, length us, event | category | flops | bytes accessed | tf_op | source)
XLA Modules:
  0.0 298.8 jit_solution(12567448268556518018)
XLA Ops:
  0.6 1.0 shard_map.51
  1.7 1.4 shard_map.52
  3.1 3.0 collective-permute-start.6
  6.0 2.2 shard_map.53
  8.2 1.0 collective-permute-start.4
  9.2 1.1 collective-permute-start.5
  10.3 1.1 slice_bitcast_fusion
  11.4 0.5 collective-permute-start.1
  11.9 1.3 fusion
  13.2 84.4 %collective-permute-done.5 = f32[8,128,128]{2,1,0:T(8,128)S(1)} collective-permute-done((f32[8,128,128]{2,1,0:T(8,128)S(1)}, f32[8,128,128]{2,1,0:T(8,128)S(1)}, u32[]{:S(2)}, u32[]{:S(2)}) %collective-permute-start.5) | collective-permute-done | bytes 524320 | tf_op jit(solution)/shard_map/ppermute | solution.py:24
  97.6 1.8 collective-permute-start.2
  99.3 2.1 collective-permute-start.3
  101.6 2.6 collective-permute-done.2.refs_9_
  104.3 4.6 %shard_map.56 = (f32[32,128,128]{2,1,0:T(8,128)S(1)}, f32[32,128]{1,0:T(8,128)S(1)}, f32[32,128]{1,0:T(8,128)S(1)}) custom-call(f32[32,128,128]{2,1,0:T(8,128)S(1)} %pad_maximum_fusion.refs_0_, f32[4,32,128,128]{3,2,1,0:T(8,128)} %refs_4_.8, f32[4,32,128,128]{3,2,1,0:T(8,128)} %refs_4_.8, f32[4,32,128,128]{3,2,1,0:T(8,128)} %refs_4_.8, ...), custom_call_target="tpu_custom_call" | custom-call | flops 10485760 | bytes 2129920 | tf_op jit(solution)/shard_map/pallas_call | solution.py:43
  108.9 1.6 collective-permute-start.11
  110.5 4.7 %shard_map.54 = (f32[32,128,128]{2,1,0:T(8,128)S(1)}, f32[32,128]{1,0:T(8,128)S(1)}, f32[32,128]{1,0:T(8,128)S(1)}) custom-call(f32[4,32,128,128]{3,2,1,0:T(8,128)} %refs_4_.8, f32[32,128,128]{2,1,0:T(8,128)S(1)} %collective-permute-done.4.refs_1_, f32[4,32,128,128]{3,2,1,0:T(8,128)} %refs_4_.8, f32[4,32,128,128]{3,2,1,0:T(8,128)} %refs_4_.8, ...), custom_call_target="tpu_custom_call" | custom-call | flops 10485760 | bytes 2129920 | tf_op jit(solution)/shard_map/pallas_call | solution.py:43
  115.3 0.5 collective-permute-start.12
  115.8 5.4 %shard_map.55 = (f32[32,128,128]{2,1,0:T(8,128)S(1)}, f32[32,128]{1,0:T(8,128)S(1)}, f32[32,128]{1,0:T(8,128)S(1)}) custom-call(f32[4,32,128,128]{3,2,1,0:T(8,128)} %refs_4_.8, f32[4,32,128,128]{3,2,1,0:T(8,128)} %refs_4_.8, f32[4,32,128,128]{3,2,1,0:T(8,128)} %refs_4_.8, f32[4,32,128,128]{3,2,1,0:T(8,128)} %refs_4_.8, f32[4,32,128,128]{3,2,1,0:T(8,128)} %refs_4_.8, ...), custom_call_target="tpu_custom_call" | custom-call | flops 10485760 | bytes 2129920 | tf_op jit(solution)/shard_map/pallas_call | solution.py:43
  121.2 5.5 %shard_map.50 = (f32[32,128,128]{2,1,0:T(8,128)S(1)}, f32[32,128]{1,0:T(8,128)S(1)}, f32[32,128]{1,0:T(8,128)S(1)}) custom-call(f32[4,32,128,128]{3,2,1,0:T(8,128)} %refs_4_.8, f32[4,32,128,128]{3,2,1,0:T(8,128)} %refs_4_.8, f32[4,32,128,128]{3,2,1,0:T(8,128)} %refs_4_.8, f32[4,32,128,128]{3,2,1,0:T(8,128)} %refs_4_.8, f32[4,32,128,128]{3,2,1,0:T(8,128)} %refs_4_.8, ...), custom_call_target="tpu_custom_call" | custom-call | flops 10485760 | bytes 2129920 | tf_op jit(solution)/shard_map/pallas_call | solution.py:43
  126.9 0.6 collective-permute-start.7
  127.5 3.1 %collective-permute-start.10 = (f32[4,32,128]{2,1,0:T(8,128)S(1)}, f32[4,32,128]{2,1,0:T(8,128)S(1)}, u32[]{:S(2)}, u32[]{:S(2)}) collective-permute-start(f32[4,32,128]{2,1,0:T(8,128)S(1)} %pad_maximum_fusion.6), channel_id=1, source_target_pairs={{0,3},{1,0},{2,1},{3,2},{4,7},{5,4},{6,5},{7,6},{8,11},{9,8},{10,9... | collective-permute-start | bytes 196616 | tf_op jit(solution)/shard_map/ppermute | solution.py:24
  130.6 2.0 collective-permute-done.10.refs_10_
  132.7 6.4 %collective-permute-done.9.refs_9_ = f32[4,32,128]{2,1,0:T(8,128)S(1)} collective-permute-done((f32[4,32,128]{2,1,0:T(8,128)S(1)}, f32[4,32,128]{2,1,0:T(8,128)S(1)}, u32[]{:S(2)}, u32[]{:S(2)}) %collective-permute-start.9) | collective-permute-done | bytes 65568 | tf_op jit(solution)/shard_map/ppermute | solution.py:24
  139.2 18.3 %collective-permute-done.11.refs_1_ = f32[32,128,128]{2,1,0:T(8,128)S(1)} collective-permute-done((f32[32,128,128]{2,1,0:T(8,128)S(1)}, f32[32,128,128]{2,1,0:T(8,128)S(1)}, u32[]{:S(2)}, u32[]{:S(2)}) %collective-permute-start.11) | collective-permute-done | bytes 2097184 | tf_op jit(solution)/shard_map/ppermute | solution.py:24
  157.5 3.3 %shard_map.58 = (f32[32,128,128]{2,1,0:T(8,128)S(1)}, f32[32,128]{1,0:T(8,128)S(1)}, f32[32,128]{1,0:T(8,128)S(1)}) custom-call(f32[32,128,128]{2,1,0:T(8,128)S(1)} %get-tuple-element.58.refs_2_.refs_3_.refs_4_.refs_0_.refs_1_, f32[32,128,128]{2,1,0:T(8,128)S(1)} %collective-permute-done.11.refs_1_, ...), custom_call_target="tpu_custom_call" | custom-call | flops 10485760 | bytes 2129920 | tf_op jit(solution)/shard_map/pallas_call | solution.py:43
  160.8 1.5 collective-permute-start.19
  162.4 3.3 %shard_map.60 = (f32[32,128,128]{2,1,0:T(8,128)S(1)}, f32[32,128]{1,0:T(8,128)S(1)}, f32[32,128]{1,0:T(8,128)S(1)}) custom-call(f32[32,128,128]{2,1,0:T(8,128)S(1)} %get-tuple-element.61.refs_2_.refs_3_.refs_4_.refs_0_, f32[32,128,128]{2,1,0:T(8,128)S(1)} %get-tuple-element.58.refs_2_.refs_3_.refs_4_.refs_0_.refs_1_, ...), custom_call_target="tpu_custom_call" | custom-call | flops 10485760 | bytes 2129920 | tf_op jit(solution)/shard_map/pallas_call | solution.py:43
  165.7 3.4 %shard_map.57 = (f32[32,128,128]{2,1,0:T(8,128)S(1)}, f32[32,128]{1,0:T(8,128)S(1)}, f32[32,128]{1,0:T(8,128)S(1)}) custom-call(f32[32,128,128]{2,1,0:T(8,128)S(1)} %get-tuple-element.53.refs_0_.refs_1_.refs_2_.refs_3_.refs_4_, f32[32,128,128]{2,1,0:T(8,128)S(1)} %get-tuple-element.57.refs_1_.refs_2_.refs_3_.refs_4_, ...), custom_call_target="tpu_custom_call" | custom-call | flops 10485760 | bytes 2129920 | tf_op jit(solution)/shard_map/pallas_call | solution.py:43
  169.2 34.2 %collective-permute-done.12.refs_0_ = f32[32,128,128]{2,1,0:T(8,128)S(1)} collective-permute-done((f32[32,128,128]{2,1,0:T(8,128)S(1)}, f32[32,128,128]{2,1,0:T(8,128)S(1)}, u32[]{:S(2)}, u32[]{:S(2)}) %collective-permute-start.12) | collective-permute-done | bytes 2097184 | tf_op jit(solution)/shard_map/ppermute | solution.py:24
  203.4 3.3 %shard_map.59 = (f32[32,128,128]{2,1,0:T(8,128)S(1)}, f32[32,128]{1,0:T(8,128)S(1)}, f32[32,128]{1,0:T(8,128)S(1)}) custom-call(f32[32,128,128]{2,1,0:T(8,128)S(1)} %collective-permute-done.12.refs_0_, f32[32,128,128]{2,1,0:T(8,128)S(1)} %get-tuple-element.53.refs_0_.refs_1_.refs_2_.refs_3_.refs_4_, ...), custom_call_target="tpu_custom_call" | custom-call | flops 10485760 | bytes 2129920 | tf_op jit(solution)/shard_map/pallas_call | solution.py:43
  207.0 0.6 collective-permute-start.18
  207.6 1.4 collective-permute-start.17
  209.0 3.1 %collective-permute-start.16 = (f32[4,32,128]{2,1,0:T(8,128)S(1)}, f32[4,32,128]{2,1,0:T(8,128)S(1)}, u32[]{:S(2)}, u32[]{:S(2)}) collective-permute-start(f32[4,32,128]{2,1,0:T(8,128)S(1)} %pad_maximum_fusion.8), channel_id=1, source_target_pairs={{0,3},{1,0},{2,1},{3,2},{4,7},{5,4},{6,5},{7,6},{8,11},{9,8},{10,9... | collective-permute-start | bytes 196616 | tf_op jit(solution)/shard_map/ppermute | solution.py:24
  212.2 1.8 collective-permute-done.16.refs_9_.refs_10_
  214.1 4.2 %collective-permute-done.15.refs_8_.refs_9_ = f32[4,32,128]{2,1,0:T(8,128)S(1)} collective-permute-done((f32[4,32,128]{2,1,0:T(8,128)S(1)}, f32[4,32,128]{2,1,0:T(8,128)S(1)}, u32[]{:S(2)}, u32[]{:S(2)}) %collective-permute-start.15) | collective-permute-done | bytes 65568 | tf_op jit(solution)/shard_map/ppermute | solution.py:24
  218.2 1.5 collective-permute-done.13.refs_6_.refs_7_
  219.8 4.8 %shard_map.62 = (f32[32,128,128]{2,1,0:T(8,128)S(1)}, f32[2,32,128]{2,1,0:T(8,128)S(1)}, f32[4,32,128,128]{3,2,1,0:T(8,128)}) custom-call(f32[32,128,128]{2,1,0:T(8,128)S(1)} %get-tuple-element.72.refs_0_.refs_2_.refs_3_.refs_4_, f32[32,128,128]{2,1,0:T(8,128)S(1)} %get-tuple-element.70.refs_0_.refs_1_.refs_2_.refs_3_.refs_4_, ...), custom_call_target="tpu_custom_call" | custom-call | flops 10485760 | bytes 10518528 | tf_op jit(solution)/shard_map/pallas_call | solution.py:43
  224.6 0.9 collective-permute-start.27
  225.5 4.9 %collective-permute-done.26.refs_2_ = f32[2,32,128]{2,1,0:T(8,128)S(1)} collective-permute-done((f32[2,32,128]{2,1,0:T(8,128)S(1)}, f32[2,32,128]{2,1,0:T(8,128)S(1)}, u32[]{:S(2)}, u32[]{:S(2)}) %collective-permute-start.26) | collective-permute-done | bytes 32800 | tf_op jit(solution)/shard_map/ppermute | solution.py:24
  230.4 4.8 %shard_map.63 = (f32[32,128,128]{2,1,0:T(8,128)S(1)}, f32[2,32,128]{2,1,0:T(8,128)S(1)}, f32[4,32,128,128]{3,2,1,0:T(8,128)}) custom-call(f32[32,128,128]{2,1,0:T(8,128)S(1)} %get-tuple-element.73.refs_2_.refs_3_.refs_4_.refs_0_, f32[32,128,128]{2,1,0:T(8,128)S(1)} %get-tuple-element.71.refs_1_.refs_2_.refs_3_, ...), custom_call_target="tpu_custom_call", output_to_operand_aliasing={{2}: (11, {})} | custom-call | flops 10485760 | bytes 10518528 | tf_op jit(solution)/shard_map/pallas_call | solution.py:43
  235.2 2.0 collective-permute-start.23
  237.3 11.1 %collective-permute-done.19.refs_1_ = f32[32,128,128]{2,1,0:T(8,128)S(1)} collective-permute-done((f32[32,128,128]{2,1,0:T(8,128)S(1)}, f32[32,128,128]{2,1,0:T(8,128)S(1)}, u32[]{:S(2)}, u32[]{:S(2)}) %collective-permute-start.19) | collective-permute-done | bytes 2097184 | tf_op jit(solution)/shard_map/ppermute | solution.py:24
  248.3 3.3 %collective-permute-start.25 = (f32[2,32,128]{2,1,0:T(8,128)S(1)}, f32[2,32,128]{2,1,0:T(8,128)S(1)}, u32[]{:S(2)}, u32[]{:S(2)}) collective-permute-start(f32[2,32,128]{2,1,0:T(8,128)S(1)} %get-tuple-element.89.refs_1_), channel_id=1, source_target_pairs={{0,3},{1,0},{2,1},{3,2},{4,7},{5,4},{6,5},{7,6},{8,11},{9,8},{10,9... | collective-permute-start | bytes 98312 | tf_op jit(solution)/shard_map/ppermute | solution.py:24
  251.7 4.8 %shard_map.64 = (f32[32,128,128]{2,1,0:T(8,128)S(1)}, f32[2,32,128]{2,1,0:T(8,128)S(1)}, f32[4,32,128,128]{3,2,1,0:T(8,128)}) custom-call(f32[32,128,128]{2,1,0:T(8,128)S(1)} %get-tuple-element.73.refs_2_.refs_3_.refs_4_.refs_0_, f32[32,128,128]{2,1,0:T(8,128)S(1)} %collective-permute-done.19.refs_1_, ...), custom_call_target="tpu_custom_call", output_to_operand_aliasing={{2}: (11, {})} | custom-call | flops 10485760 | bytes 10518528 | tf_op jit(solution)/shard_map/pallas_call | solution.py:43
  256.5 0.6 collective-permute-start.21
  257.1 3.3 %collective-permute-start.22 = (f32[2,32,128]{2,1,0:T(8,128)S(1)}, f32[2,32,128]{2,1,0:T(8,128)S(1)}, u32[]{:S(2)}, u32[]{:S(2)}) collective-permute-start(f32[2,32,128]{2,1,0:T(8,128)S(1)} %get-tuple-element.87.refs_1_), channel_id=1, source_target_pairs={{0,3},{1,0},{2,1},{3,2},{4,7},{5,4},{6,5},{7,6},{8,11},{9,8},{10,9... | collective-permute-start | bytes 98312 | tf_op jit(solution)/shard_map/ppermute | solution.py:24
  260.4 3.3 %shard_map.61 = (f32[32,128,128]{2,1,0:T(8,128)S(1)}, f32[32,128,128]{2,1,0:T(8,128)S(1)}) custom-call(f32[32,128,128]{2,1,0:T(8,128)S(1)} %get-tuple-element.70.refs_0_.refs_1_.refs_2_.refs_3_.refs_4_, f32[32,128,128]{2,1,0:T(8,128)S(1)} %get-tuple-element.71.refs_1_.refs_2_.refs_3_, f32[32,128,128]{2,1,0:T(8,128)S(1)} %get-tuple-element.71.refs_1_.refs_2_.refs_3_, ...), custom_call_target="tpu_custom_call" | custom-call | flops 10485760 | bytes 4194304 | tf_op jit(solution)/shard_map/pallas_call | solution.py:43
  263.7 2.0 shard_map.65
  265.7 1.9 shard_map.66
  267.6 2.0 shard_map.67
  270.2 1.1 collective-permute-start.29
  271.3 2.7 collective-permute-start.30
  274.0 1.1 collective-permute-start.31
  275.1 0.7 collective-permute-done.29.refs_2_
  276.0 1.7 collective-permute-done.31.refs_4_
  277.7 1.0 shard_map.69
  278.8 10.3 %collective-permute-done.17.refs_2_ = f32[16,128,128]{2,1,0:T(8,128)S(1)} collective-permute-done((f32[16,128,128]{2,1,0:T(8,128)S(1)}, f32[16,128,128]{2,1,0:T(8,128)S(1)}, u32[]{:S(2)}, u32[]{:S(2)}) %collective-permute-start.17) | collective-permute-done | bytes 1048608 | tf_op jit(solution)/shard_map/ppermute | solution.py:24
  289.4 1.4 collective-permute-start.32
  290.8 3.3 %collective-permute-start.33 = (f32[2,16,128]{2,1,0:T(8,128)S(1)}, f32[2,16,128]{2,1,0:T(8,128)S(1)}, u32[]{:S(2)}, u32[]{:S(2)}) collective-permute-start(f32[2,16,128]{2,1,0:T(8,128)S(1)} %get-tuple-element.100.refs_1_), channel_id=1, source_target_pairs={{0,2},{1,3},{2,0},{3,1},{4,6},{5,7},{6,4},{7,5},{8,10},{9,11},{10,... | collective-permute-start | bytes 49160 | tf_op jit(solution)/shard_map/ppermute | solution.py:24
  294.0 0.8 collective-permute-start.34
  294.9 1.0 shard_map.72.refs_0_
  295.9 1.0 shard_map.73
  296.9 0.9 collective-permute-done.34.refs_4_
  297.8 1.0 shard_map.71
  (49 shorter events, 2.2 us)
Async XLA Ops:
  3.1 96.3 %collective-permute-start.6 = (f32[24,128,128]{2,1,0:T(8,128)S(1)}, f32[24,128,128]{2,1,0:T(8,128)S(1)}, u32[]{:S(2)}, u32[]{:S(2)}) collective-permute-start(f32[24,128,128]{2,1,0:T(8,128)S(1)} %get-tuple-element.60), channel_id=1, source_target_pairs={{0,8},{8,16},{16,24},{24,0},{1,9},{9,17},{17,25},{25,1},{2,10},{10... | collective-permute-start | bytes 4718600 | tf_op jit(solution)/shard_map/ppermute | solution.py:24
  8.2 102.3 %collective-permute-start.4 = (f32[32,128,128]{2,1,0:T(8,128)S(1)}, f32[32,128,128]{2,1,0:T(8,128)S(1)}, u32[]{:S(2)}, u32[]{:S(2)}) collective-permute-start(f32[32,128,128]{2,1,0:T(8,128)S(1)} %get-tuple-element.56), channel_id=1, source_target_pairs={{0,24},{8,0},{16,8},{24,16},{1,25},{9,1},{17,9},{25,17},{2,26},{10... | collective-permute-start | bytes 6291464 | tf_op jit(solution)/shard_map/ppermute | solution.py:24
  9.2 88.4 %collective-permute-start.5 = (f32[8,128,128]{2,1,0:T(8,128)S(1)}, f32[8,128,128]{2,1,0:T(8,128)S(1)}, u32[]{:S(2)}, u32[]{:S(2)}) collective-permute-start(f32[8,128,128]{2,1,0:T(8,128)S(1)} %get-tuple-element.59), channel_id=1, source_target_pairs={{0,8},{8,16},{16,24},{24,0},{1,9},{9,17},{17,25},{25,1},{2,10},{10... | collective-permute-start | bytes 1572872 | tf_op jit(solution)/shard_map/ppermute | solution.py:24
  11.3 93.0 %collective-permute-start = (f32[4,128,128]{2,1,0:T(8,128)S(1)}, f32[4,128,128]{2,1,0:T(8,128)S(1)}, u32[]{:S(2)}, u32[]{:S(2)}) collective-permute-start(f32[4,128,128]{2,1,0:T(8,128)S(1)} %get-tuple-element.107), channel_id=1, source_target_pairs={{0,4},{4,0},{1,5},{5,1},{2,6},{6,2},{3,7},{7,3},{8,12},{12,8},{9,1... | collective-permute-start | bytes 786440 | tf_op jit(solution)/shard_map/ppermute | solution.py:24
  11.4 92.9 %collective-permute-start.1 = (f32[4,128,128]{2,1,0:T(8,128)S(1)}, f32[4,128,128]{2,1,0:T(8,128)S(1)}, u32[]{:S(2)}, u32[]{:S(2)}) collective-permute-start(f32[4,128,128]{2,1,0:T(8,128)S(1)} %get-tuple-element.106), channel_id=1, source_target_pairs={{0,4},{4,0},{1,5},{5,1},{2,6},{6,2},{3,7},{7,3},{8,12},{12,8},{9,1... | collective-permute-start | bytes 786440 | tf_op jit(solution)/shard_map/ppermute | solution.py:24
  97.6 6.6 %collective-permute-start.2 = (f32[4,32,128]{2,1,0:T(8,128)S(1)}, f32[4,32,128]{2,1,0:T(8,128)S(1)}, u32[]{:S(2)}, u32[]{:S(2)}) collective-permute-start(f32[4,32,128]{2,1,0:T(8,128)S(1)} %bitcast.47), channel_id=1, source_target_pairs={{0,1},{1,2},{2,3},{3,0},{4,5},{5,6},{6,7},{7,4},{8,9},{9,10},{10,1... | collective-permute-start | bytes 196616 | tf_op jit(solution)/shard_map/ppermute | solution.py:24
  99.3 5.0 %collective-permute-start.3 = (f32[4,32,128]{2,1,0:T(8,128)S(1)}, f32[4,32,128]{2,1,0:T(8,128)S(1)}, u32[]{:S(2)}, u32[]{:S(2)}) collective-permute-start(f32[4,32,128]{2,1,0:T(8,128)S(1)} %bitcast.46), channel_id=1, source_target_pairs={{0,3},{1,0},{2,1},{3,2},{4,7},{5,4},{6,5},{7,6},{8,11},{9,8},{10,9... | collective-permute-start | bytes 196616 | tf_op jit(solution)/shard_map/ppermute | solution.py:24
  108.9 48.6 %collective-permute-start.11 = (f32[32,128,128]{2,1,0:T(8,128)S(1)}, f32[32,128,128]{2,1,0:T(8,128)S(1)}, u32[]{:S(2)}, u32[]{:S(2)}) collective-permute-start(f32[32,128,128]{2,1,0:T(8,128)S(1)} %get-tuple-element.61.refs_2_.refs_3_.refs_4_.refs_0_), channel_id=1, source_target_pairs={{0,24},{8,0},{16,8},{24,16},{1,25},{9,1},{17,9},{25,17},{2,26},{10... | collective-permute-start | bytes 6291464 | tf_op jit(solution)/shard_map/ppermute | solution.py:24
  115.3 88.1 %collective-permute-start.12 = (f32[32,128,128]{2,1,0:T(8,128)S(1)}, f32[32,128,128]{2,1,0:T(8,128)S(1)}, u32[]{:S(2)}, u32[]{:S(2)}) collective-permute-start(f32[32,128,128]{2,1,0:T(8,128)S(1)} %get-tuple-element.57.refs_1_.refs_2_.refs_3_.refs_4_), channel_id=1, source_target_pairs={{0,8},{8,16},{16,24},{24,0},{1,9},{9,17},{17,25},{25,1},{2,10},{10... | collective-permute-start | bytes 6291464 | tf_op jit(solution)/shard_map/ppermute | solution.py:24
  126.8 12.4 %collective-permute-start.8 = (f32[4,128,128]{2,1,0:T(8,128)S(1)}, f32[4,128,128]{2,1,0:T(8,128)S(1)}, u32[]{:S(2)}, u32[]{:S(2)}) collective-permute-start(f32[4,128,128]{2,1,0:T(8,128)S(1)} %pad_maximum_fusion.2), channel_id=1, source_target_pairs={{0,4},{4,0},{1,5},{5,1},{2,6},{6,2},{3,7},{7,3},{8,12},{12,8},{9,1... | collective-permute-start | bytes 786440 | tf_op jit(solution)/shard_map/ppermute | solution.py:24
  126.9 12.3 %collective-permute-start.7 = (f32[4,128,128]{2,1,0:T(8,128)S(1)}, f32[4,128,128]{2,1,0:T(8,128)S(1)}, u32[]{:S(2)}, u32[]{:S(2)}) collective-permute-start(f32[4,128,128]{2,1,0:T(8,128)S(1)} %pad_maximum_fusion.1), channel_id=1, source_target_pairs={{0,4},{4,0},{1,5},{5,1},{2,6},{6,2},{3,7},{7,3},{8,12},{12,8},{9,1... | collective-permute-start | bytes 786440 | tf_op jit(solution)/shard_map/ppermute | solution.py:24
  127.5 5.2 %collective-permute-start.10 = (f32[4,32,128]{2,1,0:T(8,128)S(1)}, f32[4,32,128]{2,1,0:T(8,128)S(1)}, u32[]{:S(2)}, u32[]{:S(2)}) collective-permute-start(f32[4,32,128]{2,1,0:T(8,128)S(1)} %pad_maximum_fusion.6), channel_id=1, source_target_pairs={{0,3},{1,0},{2,1},{3,2},{4,7},{5,4},{6,5},{7,6},{8,11},{9,8},{10,9... | collective-permute-start | bytes 196616 | tf_op jit(solution)/shard_map/ppermute | solution.py:24
  132.7 6.5 %collective-permute-start.9 = (f32[4,32,128]{2,1,0:T(8,128)S(1)}, f32[4,32,128]{2,1,0:T(8,128)S(1)}, u32[]{:S(2)}, u32[]{:S(2)}) collective-permute-start(f32[4,32,128]{2,1,0:T(8,128)S(1)} %pad_maximum_fusion.5), channel_id=1, source_target_pairs={{0,1},{1,2},{2,3},{3,0},{4,5},{5,6},{6,7},{7,4},{8,9},{9,10},{10,1... | collective-permute-start | bytes 196616 | tf_op jit(solution)/shard_map/ppermute | solution.py:24
  160.8 87.5 %collective-permute-start.19 = (f32[32,128,128]{2,1,0:T(8,128)S(1)}, f32[32,128,128]{2,1,0:T(8,128)S(1)}, u32[]{:S(2)}, u32[]{:S(2)}) collective-permute-start(f32[32,128,128]{2,1,0:T(8,128)S(1)} %get-tuple-element.71.refs_1_.refs_2_.refs_3_), channel_id=1, source_target_pairs={{0,8},{8,16},{16,24},{24,0},{1,9},{9,17},{17,25},{25,1},{2,10},{10... | collective-permute-start | bytes 6291464 | tf_op jit(solution)/shard_map/ppermute | solution.py:24
  207.0 62.9 %collective-permute-start.18 = (f32[16,128,128]{2,1,0:T(8,128)S(1)}, f32[16,128,128]{2,1,0:T(8,128)S(1)}, u32[]{:S(2)}, u32[]{:S(2)}) collective-permute-start(f32[16,128,128]{2,1,0:T(8,128)S(1)} %get-tuple-element.108), channel_id=1, source_target_pairs={{0,24},{8,0},{16,8},{24,16},{1,25},{9,1},{17,9},{25,17},{2,26},{10... | collective-permute-start | bytes 3145736 | tf_op jit(solution)/shard_map/ppermute | solution.py:24
  207.6 81.5 %collective-permute-start.17 = (f32[16,128,128]{2,1,0:T(8,128)S(1)}, f32[16,128,128]{2,1,0:T(8,128)S(1)}, u32[]{:S(2)}, u32[]{:S(2)}) collective-permute-start(f32[16,128,128]{2,1,0:T(8,128)S(1)} %get-tuple-element.109), channel_id=1, source_target_pairs={{0,24},{8,0},{16,8},{24,16},{1,25},{9,1},{17,9},{25,17},{2,26},{10... | collective-permute-start | bytes 3145736 | tf_op jit(solution)/shard_map/ppermute | solution.py:24
  209.0 5.1 %collective-permute-start.16 = (f32[4,32,128]{2,1,0:T(8,128)S(1)}, f32[4,32,128]{2,1,0:T(8,128)S(1)}, u32[]{:S(2)}, u32[]{:S(2)}) collective-permute-start(f32[4,32,128]{2,1,0:T(8,128)S(1)} %pad_maximum_fusion.8), channel_id=1, source_target_pairs={{0,3},{1,0},{2,1},{3,2},{4,7},{5,4},{6,5},{7,6},{8,11},{9,8},{10,9... | collective-permute-start | bytes 196616 | tf_op jit(solution)/shard_map/ppermute | solution.py:24
  212.2 6.1 %collective-permute-start.15 = (f32[4,32,128]{2,1,0:T(8,128)S(1)}, f32[4,32,128]{2,1,0:T(8,128)S(1)}, u32[]{:S(2)}, u32[]{:S(2)}) collective-permute-start(f32[4,32,128]{2,1,0:T(8,128)S(1)} %pad_maximum_fusion.7), channel_id=1, source_target_pairs={{0,1},{1,2},{2,3},{3,0},{4,5},{5,6},{6,7},{7,4},{8,9},{9,10},{10,1... | collective-permute-start | bytes 196616 | tf_op jit(solution)/shard_map/ppermute | solution.py:24
  214.1 4.2 %collective-permute-start.14 = (f32[4,128,128]{2,1,0:T(8,128)S(1)}, f32[4,128,128]{2,1,0:T(8,128)S(1)}, u32[]{:S(2)}, u32[]{:S(2)}) collective-permute-start(f32[4,128,128]{2,1,0:T(8,128)S(1)} %pad_maximum_fusion.4), channel_id=1, source_target_pairs={{0,4},{4,0},{1,5},{5,1},{2,6},{6,2},{3,7},{7,3},{8,12},{12,8},{9,1... | collective-permute-start | bytes 786440 | tf_op jit(solution)/shard_map/ppermute | solution.py:24
  218.2 1.5 collective-permute-start.13
  224.6 5.9 %collective-permute-start.26 = (f32[2,32,128]{2,1,0:T(8,128)S(1)}, f32[2,32,128]{2,1,0:T(8,128)S(1)}, u32[]{:S(2)}, u32[]{:S(2)}) collective-permute-start(f32[2,32,128]{2,1,0:T(8,128)S(1)} %get-tuple-element.91.refs_1_), channel_id=1, source_target_pairs={{0,1},{1,2},{2,3},{3,0},{4,5},{5,6},{6,7},{7,4},{8,9},{9,10},{10,1... | collective-permute-start | bytes 98312 | tf_op jit(solution)/shard_map/ppermute | solution.py:24
  224.6 10.7 %collective-permute-start.27 = (f32[2,32,128]{2,1,0:T(8,128)S(1)}, f32[2,32,128]{2,1,0:T(8,128)S(1)}, u32[]{:S(2)}, u32[]{:S(2)}) collective-permute-start(f32[2,32,128]{2,1,0:T(8,128)S(1)} %get-tuple-element.91.refs_1_), channel_id=1, source_target_pairs={{0,2},{1,3},{2,0},{3,1},{4,6},{5,7},{6,4},{7,5},{8,10},{9,11},{10,... | collective-permute-start | bytes 98312 | tf_op jit(solution)/shard_map/ppermute | solution.py:24
  230.4 6.8 %collective-permute-start.28 = (f32[2,32,128]{2,1,0:T(8,128)S(1)}, f32[2,32,128]{2,1,0:T(8,128)S(1)}, u32[]{:S(2)}, u32[]{:S(2)}) collective-permute-start(f32[2,32,128]{2,1,0:T(8,128)S(1)} %get-tuple-element.91.refs_1_), channel_id=1, source_target_pairs={{0,3},{1,0},{2,1},{3,2},{4,7},{5,4},{6,5},{7,6},{8,11},{9,8},{10,9... | collective-permute-start | bytes 98312 | tf_op jit(solution)/shard_map/ppermute | solution.py:24
  235.2 21.3 %collective-permute-start.23 = (f32[2,32,128]{2,1,0:T(8,128)S(1)}, f32[2,32,128]{2,1,0:T(8,128)S(1)}, u32[]{:S(2)}, u32[]{:S(2)}) collective-permute-start(f32[2,32,128]{2,1,0:T(8,128)S(1)} %get-tuple-element.89.refs_1_), channel_id=1, source_target_pairs={{0,1},{1,2},{2,3},{3,0},{4,5},{5,6},{6,7},{7,4},{8,9},{9,10},{10,1... | collective-permute-start | bytes 98312 | tf_op jit(solution)/shard_map/ppermute | solution.py:24
  237.3 19.2 %collective-permute-start.24 = (f32[2,32,128]{2,1,0:T(8,128)S(1)}, f32[2,32,128]{2,1,0:T(8,128)S(1)}, u32[]{:S(2)}, u32[]{:S(2)}) collective-permute-start(f32[2,32,128]{2,1,0:T(8,128)S(1)} %get-tuple-element.89.refs_1_), channel_id=1, source_target_pairs={{0,2},{1,3},{2,0},{3,1},{4,6},{5,7},{6,4},{7,5},{8,10},{9,11},{10,... | collective-permute-start | bytes 98312 | tf_op jit(solution)/shard_map/ppermute | solution.py:24
  248.3 8.7 %collective-permute-start.25 = (f32[2,32,128]{2,1,0:T(8,128)S(1)}, f32[2,32,128]{2,1,0:T(8,128)S(1)}, u32[]{:S(2)}, u32[]{:S(2)}) collective-permute-start(f32[2,32,128]{2,1,0:T(8,128)S(1)} %get-tuple-element.89.refs_1_), channel_id=1, source_target_pairs={{0,3},{1,0},{2,1},{3,2},{4,7},{5,4},{6,5},{7,6},{8,11},{9,8},{10,9... | collective-permute-start | bytes 98312 | tf_op jit(solution)/shard_map/ppermute | solution.py:24
  256.5 11.1 %collective-permute-start.20 = (f32[2,32,128]{2,1,0:T(8,128)S(1)}, f32[2,32,128]{2,1,0:T(8,128)S(1)}, u32[]{:S(2)}, u32[]{:S(2)}) collective-permute-start(f32[2,32,128]{2,1,0:T(8,128)S(1)} %get-tuple-element.87.refs_1_), channel_id=1, source_target_pairs={{0,1},{1,2},{2,3},{3,0},{4,5},{5,6},{6,7},{7,4},{8,9},{9,10},{10,1... | collective-permute-start | bytes 98312 | tf_op jit(solution)/shard_map/ppermute | solution.py:24
  256.5 11.1 %collective-permute-start.21 = (f32[2,32,128]{2,1,0:T(8,128)S(1)}, f32[2,32,128]{2,1,0:T(8,128)S(1)}, u32[]{:S(2)}, u32[]{:S(2)}) collective-permute-start(f32[2,32,128]{2,1,0:T(8,128)S(1)} %get-tuple-element.87.refs_1_), channel_id=1, source_target_pairs={{0,2},{1,3},{2,0},{3,1},{4,6},{5,7},{6,4},{7,5},{8,10},{9,11},{10,... | collective-permute-start | bytes 98312 | tf_op jit(solution)/shard_map/ppermute | solution.py:24
  257.1 10.5 %collective-permute-start.22 = (f32[2,32,128]{2,1,0:T(8,128)S(1)}, f32[2,32,128]{2,1,0:T(8,128)S(1)}, u32[]{:S(2)}, u32[]{:S(2)}) collective-permute-start(f32[2,32,128]{2,1,0:T(8,128)S(1)} %get-tuple-element.87.refs_1_), channel_id=1, source_target_pairs={{0,3},{1,0},{2,1},{3,2},{4,7},{5,4},{6,5},{7,6},{8,11},{9,8},{10,9... | collective-permute-start | bytes 98312 | tf_op jit(solution)/shard_map/ppermute | solution.py:24
  270.2 5.6 %collective-permute-start.29 = (f32[2,16,128]{2,1,0:T(8,128)S(1)}, f32[2,16,128]{2,1,0:T(8,128)S(1)}, u32[]{:S(2)}, u32[]{:S(2)}) collective-permute-start(f32[2,16,128]{2,1,0:T(8,128)S(1)} %get-tuple-element.96.refs_1_), channel_id=1, source_target_pairs={{0,1},{1,2},{2,3},{3,0},{4,5},{5,6},{6,7},{7,4},{8,9},{9,10},{10,1... | collective-permute-start | bytes 49160 | tf_op jit(solution)/shard_map/ppermute | solution.py:24
  271.3 4.7 %collective-permute-start.30 = (f32[2,16,128]{2,1,0:T(8,128)S(1)}, f32[2,16,128]{2,1,0:T(8,128)S(1)}, u32[]{:S(2)}, u32[]{:S(2)}) collective-permute-start(f32[2,16,128]{2,1,0:T(8,128)S(1)} %get-tuple-element.96.refs_1_), channel_id=1, source_target_pairs={{0,2},{1,3},{2,0},{3,1},{4,6},{5,7},{6,4},{7,5},{8,10},{9,11},{10,... | collective-permute-start | bytes 49160 | tf_op jit(solution)/shard_map/ppermute | solution.py:24
  274.0 3.7 %collective-permute-start.31 = (f32[2,16,128]{2,1,0:T(8,128)S(1)}, f32[2,16,128]{2,1,0:T(8,128)S(1)}, u32[]{:S(2)}, u32[]{:S(2)}) collective-permute-start(f32[2,16,128]{2,1,0:T(8,128)S(1)} %get-tuple-element.96.refs_1_), channel_id=1, source_target_pairs={{0,3},{1,0},{2,1},{3,2},{4,7},{5,4},{6,5},{7,6},{8,11},{9,8},{10,9... | collective-permute-start | bytes 49160 | tf_op jit(solution)/shard_map/ppermute | solution.py:24
  289.4 7.5 %collective-permute-start.32 = (f32[2,16,128]{2,1,0:T(8,128)S(1)}, f32[2,16,128]{2,1,0:T(8,128)S(1)}, u32[]{:S(2)}, u32[]{:S(2)}) collective-permute-start(f32[2,16,128]{2,1,0:T(8,128)S(1)} %get-tuple-element.100.refs_1_), channel_id=1, source_target_pairs={{0,1},{1,2},{2,3},{3,0},{4,5},{5,6},{6,7},{7,4},{8,9},{9,10},{10,1... | collective-permute-start | bytes 49160 | tf_op jit(solution)/shard_map/ppermute | solution.py:24
  290.8 6.1 %collective-permute-start.33 = (f32[2,16,128]{2,1,0:T(8,128)S(1)}, f32[2,16,128]{2,1,0:T(8,128)S(1)}, u32[]{:S(2)}, u32[]{:S(2)}) collective-permute-start(f32[2,16,128]{2,1,0:T(8,128)S(1)} %get-tuple-element.100.refs_1_), channel_id=1, source_target_pairs={{0,2},{1,3},{2,0},{3,1},{4,6},{5,7},{6,4},{7,5},{8,10},{9,11},{10,... | collective-permute-start | bytes 49160 | tf_op jit(solution)/shard_map/ppermute | solution.py:24
  294.0 3.7 %collective-permute-start.34 = (f32[2,16,128]{2,1,0:T(8,128)S(1)}, f32[2,16,128]{2,1,0:T(8,128)S(1)}, u32[]{:S(2)}, u32[]{:S(2)}) collective-permute-start(f32[2,16,128]{2,1,0:T(8,128)S(1)} %get-tuple-element.100.refs_1_), channel_id=1, source_target_pairs={{0,3},{1,0},{2,1},{3,2},{4,7},{5,4},{6,5},{7,6},{8,11},{9,8},{10,9... | collective-permute-start | bytes 49160 | tf_op jit(solution)/shard_map/ppermute | solution.py:24
